TPU v7x, 32 devices: a whole 2x2x4 slice. The times are simulated.
32 devices in a mesh: row: 8 (over z, core), col: 4 (over y, x).
Axes of the slice: x: 2, y: 2, z: 4, core: 2. Of those that a mesh axis runs over, the one named last changes fastest.
Arguments:
- vectors: bfloat16 [2, 4, 16384], P(None, 'col', 'row'), may hold values from -6 to 6
- lr_left: bfloat16 [8, 4, 32, 8, 2048], P('row', 'col'), may hold values from -0.75 to 0.75
- lr_right: bfloat16 [8, 4, 32, 8, 2048], P('row', 'col'), may hold values from -0.125 to 0.125
- tile_rank: int32 [8, 4, 32], P('row', 'col'), may hold values from 0 to 8, as said below
- leaf_values: bfloat16 [8, 4, 8, 512, 512], P('row', 'col'), may hold values from -0.25 to 0.25
- leaf_places: int32 [8, 4, 8, 2], P('row', 'col'), may hold values from 0 to 31, as said below
- cluster_perm: int32 [8, 8192], P('row'), may hold values from 0 to 65535, as said below
- kappa: float32 [32, 16, 128], P('row', 'col'), may hold values from 0.25 to 4
Outputs:
- prior_action: float32 [2, 32, 16, 128], P(None, 'row', 'col')
Inputs may be any that keep to these rules, and one draw needn't show every extreme that they name: `tile_rank`: 0 exactly on the tiles that contain a leaf, 1 to 8 on the others. `leaf_places`: the 8 leaves of a block are distinct; entry 0 indexes rows and entry 1 column of the block in units of 512. `cluster_perm`: a permutation of all brick indices; within each aligned block of 2048 entries, every value of entry // 2048 occurs exactly 128 times or not at all.
All inputs are finite; a program needn't handle non-finite values.
Results may differ from a plain program's by a relative error of at most 0.0023.
Values may be sent and summed in bfloat16 or wider, within the bound.
A program may use at most 64 MiB of HBM per device.

v0:
```python
import jax
import jax.numpy as jnp
from jax import lax
from jax.sharding import PartitionSpec as P

NVEC = 2
CX = 4
CY = 4
NZ = 128
TILE_ROWS = 4
TILE_COLS = 8
KMAX = 8
LEAF = 512


def extended(cells, sides, width):
    for axis, dim in sides:
        count = lax.axis_size(axis)
        ends = count - 1
        head = lax.slice_in_dim(cells, 0, width, axis=dim)
        tail = lax.slice_in_dim(cells, cells.shape[dim] - width, cells.shape[dim], axis=dim)
        cells = jnp.concatenate(
            [
                lax.ppermute(tail, axis, [(i, (i + 1) % count) for i in range(ends)]),
                cells,
                lax.ppermute(head, axis, [((i + 1) % count, i) for i in range(ends)]),
            ],
            axis=dim,
        )
    return cells


def prior_step(padded, stiffness):
    center = padded[:, 1:-1, 1:-1, :]
    flat_pad = jnp.pad(center, ((0, 0), (0, 0), (0, 0), (1, 1)))
    beside = padded[:, 2:, 1:-1, :] + padded[:, :-2, 1:-1, :]
    beside = beside + padded[:, 1:-1, 2:, :] + padded[:, 1:-1, :-2, :]
    beside = beside + flat_pad[..., 2:] + flat_pad[..., :-2]
    return ((6.0 + stiffness) * center - beside) * 0.125


def route(values, targets, groups, points, capacity, devices):
    target_dev = targets // points
    places = targets % points
    grouped = target_dev.reshape(groups, points)
    one_hot = (grouped[:, :, None] == jnp.arange(devices)[None, None, :]).astype(jnp.int32)
    running = jnp.cumsum(one_hot, axis=1)
    within = jnp.sum(running * one_hot, axis=2) - 1
    slot_index = jnp.arange(groups)[:, None] * capacity + within
    buffer_at = (grouped * (groups * capacity) + slot_index).reshape(-1)
    buffer_len = devices * groups * capacity
    send_values = jnp.zeros((values.shape[0], buffer_len), jnp.float32).at[:, buffer_at].set(values)
    send_places = jnp.full((1, buffer_len), points, jnp.int32).at[0, buffer_at].set(places)
    return (send_values, send_places)


def per_device(
    vectors, lr_left, lr_right, tile_rank, leaf_values, leaf_places, cluster_perm, kappa
):
    gathered = lax.all_gather(vectors, "row", axis=2, tiled=True)
    x_column = gathered[:, 0, :]
    tile_size = lr_left.shape[-1]
    rows_len = tile_size * TILE_ROWS
    x_tiles = x_column.reshape(NVEC, TILE_COLS, tile_size)
    far_right = lr_right[0, 0].reshape(TILE_ROWS, TILE_COLS, KMAX, tile_size)
    projected = jnp.einsum("abkp,vbp->abvk", far_right, x_tiles, preferred_element_type=jnp.float32)
    rank_mask = (
        jnp.arange(KMAX)[None, None, :] < tile_rank[0, 0].reshape(TILE_ROWS, TILE_COLS)[:, :, None]
    ).astype(jnp.float32)
    projected = (projected * rank_mask[:, :, None, :]).astype(jnp.bfloat16)
    far_left = lr_left[0, 0].reshape(TILE_ROWS, TILE_COLS, KMAX, tile_size)
    far_part = jnp.einsum(
        "abkp,abvk->vap", far_left, projected, preferred_element_type=jnp.float32
    ).reshape(NVEC, rows_len)
    leaf_pos = leaf_places[0, 0]
    x_sub = x_column.reshape(NVEC, x_column.shape[1] // LEAF, LEAF)
    picked = jnp.take(x_sub, leaf_pos[:, 1], axis=1)
    near_out = jnp.einsum(
        "lqp,vlp->vlq", leaf_values[0, 0], picked, preferred_element_type=jnp.float32
    )
    selector = (leaf_pos[:, 0][:, None] == jnp.arange(rows_len // LEAF)[None, :]).astype(
        jnp.float32
    )
    near_part = jnp.einsum("vlq,lr->vrq", near_out, selector, precision=lax.Precision.HIGHEST)
    partial_sums = far_part + near_part.reshape(NVEC, rows_len)
    points = vectors.shape[2]
    devices = lax.axis_size("row") * lax.axis_size("col")
    capacity = 2 * points // devices
    summed = lax.psum_scatter(partial_sums, "col", scatter_dimension=1, tiled=True)
    targets = lax.dynamic_slice_in_dim(cluster_perm[0], lax.axis_index("col") * points, points)
    send_values, send_places = route(summed, targets, 1, points, capacity, devices)
    received_values, received_places = (
        lax.all_to_all(send_values, ("row", "col"), split_axis=1, concat_axis=1, tiled=True),
        lax.all_to_all(send_places, ("row", "col"), split_axis=1, concat_axis=1, tiled=True),
    )
    field = (
        jnp.zeros((NVEC, points + 1), jnp.float32).at[:, received_places[0]].add(received_values)
    )
    field = field[:, :points].reshape(NVEC, CX, CY, NZ)
    for repeat in range(4):
        padded = extended(field, (("row", 1), ("col", 2)), 1)
        field = prior_step(padded, kappa)
    return field


def solution(mesh):
    in_specs = (
        P(None, "col", "row"),
        P("row", "col", None, None, None),
        P("row", "col", None, None, None),
        P("row", "col", None),
        P("row", "col", None, None, None),
        P("row", "col", None, None),
        P("row", None),
        P("row", "col", None),
    )
    out_specs = P(None, "row", "col", None)
    return jax.shard_map(
        per_device, mesh=mesh, in_specs=in_specs, out_specs=out_specs, check_vma=False
    )
```

profile of v0, /device:TPU:12, one launch (start us, length us, event | category | flops | bytes accessed | tf_op | source)
XLA Modules:
  0.0 208.1 jit_solution(8211785777179416884)
XLA Ops:
  8.0 14.4 %all_gather.3 = bf16[2,1,16384]{2,0,1:T(2,128)(2,1)S(1)} all-gather(bf16[2,1,2048]{2,0,1:T(2,128)(2,1)} %param.8), channel_id=1, replica_groups=mesh['row'=8,'col'=4] {'row'}, dimensions={2}, use_global_device_ids=true | all-gather | bytes 73728 | tf_op jit(solution)/shard_map/all_gather | solution.py:60
  23.1 3.5 %fusion.2 = f32[2,8,512]{2,0,1:T(2,128)S(1)} fusion(bf16[1,1,8,512,512]{4,3,2,1,0:T(8,128)(2,1)} %param.12, bf16[8,2,512]{2,1,0:T(2,128)(2,1)S(1)} %gather_fusion, pred[8]{0:T(512)(128)(4,1)S(1)} %and_bitcast_fusion), kind=kOutput, calls=%fused_computation.7 | convolution fusion | flops 8396800 | bytes 4243464 | tf_op jit(solution)/shard_map/lqp,vlp->vlq/dot_general | solution.py:78
  28.2 2.8 %fusion.7 = f32[4,2,2048,1]{2,1,3,0:T(2,128)S(1)} fusion(bf16[4,8,8,2048]{3,2,1,0:T(8,128)(2,1)S(1)} %bitcast.79, bf16[2,8,2048,1]{2,0,1,3:T(2,128)(2,1)S(1)} %bitcast.87, bf16[4,8,8,2048]{3,2,1,0:T(8,128)(2,1)S(1)} %bitcast.84, f32[4,8,8]{2,1,0:T(8,128)S(1)} %fusion.42), kind=kOutput, calls=%fused_computation.11 | convolution fusion | flops 4195328 | bytes 2229248 | tf_op jit(solution)/shard_map/abkp,abvk->vap/dot_general | solution.py:72
  31.0 2.7 %copy.53 = f32[2,8192]{0,1:T(8,128)} copy(f32[2,8192]{1,0:T(2,128)S(1)} %add.151) | data formatting | bytes 131072
  34.5 9.1 %reduce-window.6 = s32[1,32,16,128]{3,2,1,0:T(8,128)S(1)} reduce-window(s32[1,32,16,128]{3,2,1,0:T(8,128)S(1)} %bitcast.83, s32[]{:T(128)} %constant.61.clone.1), window={size=1x1x1x128 pad=0_0x0_0x0_0x127_0}, to_apply=%region_0.1 | reduce-window | flops 8323072 | bytes 524292 | tf_op jit(solution)/shard_map/reduce-window
  44.8 8.6 %scatter_custom_fusion.2 = s32[4096]{0:T(1024)} fusion(s32[2048]{0:T(1024)S(1)} %broadcast_select_fusion.2, s32[2048]{0:T(1024)S(1)} %get-tuple-element.29, s32[]{:T(128)} %constant.60.clone.1), kind=kCustom, calls=%fused_computation.107 | custom fusion | bytes 16388
  53.4 5.8 %all-to-all-start = ((s32[1,32,128]{2,0,1:T(1,128)}), s32[1,32,128]{2,0,1:T(1,128)S(1)}, u32[]{:S(2)}, u32[]{:S(2)}) async-start(s32[1,32,128]{2,0,1:T(1,128)} %bitcast.7), calls=%async_computation | async-start | bytes 32768 | tf_op jit(solution)/shard_map/all_to_all | solution.py:94
  59.2 28.3 %reduce-scatter.4.cloned.1.call-done = f32[2048,2]{1,0:T(8,128)} async-done(((f32[8192,2]{1,0:T(8,128)}), f32[2048,2]{1,0:T(8,128)}) %reduce-scatter.4.cloned.1.call-update) | async-done | bytes 16400
  90.5 6.5 %scatter_custom_fusion = f32[2,4096]{0,1:T(8,128)S(1)} fusion(s32[2048]{0:T(1024)S(1)} %bitcast.91, f32[2048,2]{1,0:T(8,128)} %copy.42, f32[]{:T(128)} %constant.59.clone.1), kind=kCustom, calls=%fused_computation.12 | custom fusion | bytes 33280 | tf_op jit(solution)/shard_map/scatter | solution.py:52
  98.1 4.9 %all-to-all-start.1 = ((f32[2,32,128]{2,0,1:T(2,128)}), f32[2,32,128]{2,0,1:T(2,128)S(1)}, u32[]{:S(2)}, u32[]{:S(2)}) async-start(f32[2,32,128]{2,0,1:T(2,128)} %copy.43), calls=%async_computation.1 | async-start | bytes 65536 | tf_op jit(solution)/shard_map/all_to_all | solution.py:93
  103.1 5.1 %all-to-all-done.1 = f32[2,32,128]{2,0,1:T(2,128)S(1)} async-done(((f32[2,32,128]{2,0,1:T(2,128)}), f32[2,32,128]{2,0,1:T(2,128)S(1)}, u32[]{:S(2)}, u32[]{:S(2)}) %all-to-all-start.1) | async-done | bytes 32800 | tf_op jit(solution)/shard_map/all_to_all | solution.py:93
  110.2 26.0 %scatter_custom_fusion.1 = f32[2,2049]{0,1:T(8,128)S(1)} fusion(s32[4096]{0:T(1024)S(1)} %bitcast.96, f32[4096,2]{1,0:T(8,128)} %copy.44, f32[]{:T(128)} %constant.59.clone.1), kind=kCustom, calls=%fused_computation.14 | custom fusion | flops 8192 | bytes 16904 | tf_op jit(solution)/shard_map/scatter-add | solution.py:97
  136.6 3.0 %collective-permute-start = (f32[2,1,4,128]{3,2,1,0:T(4,128)S(1)}, f32[2,1,4,128]{3,2,1,0:T(4,128)S(1)}, u32[]{:S(2)}, u32[]{:S(2)}) collective-permute-start(f32[2,1,4,128]{3,2,1,0:T(4,128)S(1)} %get-tuple-element.26), channel_id=1, source_target_pairs={{4,0},{8,4},{12,8},{16,12},{20,16},{24,20},{28,24},{5,1},{9,5},{13... | collective-permute-start | bytes 12296 | tf_op jit(solution)/shard_map/ppermute | solution.py:26
  141.5 3.0 %collective-permute-done.1 = f32[2,1,4,128]{3,2,1,0:T(4,128)S(1)} collective-permute-done((f32[2,1,4,128]{3,2,1,0:T(4,128)S(1)}, f32[2,1,4,128]{3,2,1,0:T(4,128)S(1)}, u32[]{:S(2)}, u32[]{:S(2)}) %collective-permute-start.1) | collective-permute-done | bytes 4128 | tf_op jit(solution)/shard_map/ppermute | solution.py:24
  144.5 3.4 %collective-permute-start.2 = (f32[2,6,1,128]{3,2,1,0:T(1,128)S(1)}, f32[2,6,1,128]{3,2,1,0:T(1,128)S(1)}, u32[]{:S(2)}, u32[]{:S(2)}) collective-permute-start(f32[2,6,1,128]{3,2,1,0:T(1,128)S(1)} %get-tuple-element.17), channel_id=1, source_target_pairs={{1,0},{2,1},{3,2},{5,4},{6,5},{7,6},{9,8},{10,9},{11,10},{13,12},{... | collective-permute-start | bytes 18440 | tf_op jit(solution)/shard_map/ppermute | solution.py:26
  147.8 2.5 %collective-permute-start.3 = (f32[2,6,1,128]{3,2,1,0:T(1,128)S(1)}, f32[2,6,1,128]{3,2,1,0:T(1,128)S(1)}, u32[]{:S(2)}, u32[]{:S(2)}) collective-permute-start(f32[2,6,1,128]{3,2,1,0:T(1,128)S(1)} %get-tuple-element.18), channel_id=1, source_target_pairs={{0,1},{1,2},{2,3},{4,5},{5,6},{6,7},{8,9},{9,10},{10,11},{12,13},{... | collective-permute-start | bytes 18440 | tf_op jit(solution)/shard_map/ppermute | solution.py:24
  150.4 3.9 %collective-permute-done.3 = f32[2,6,1,128]{3,2,1,0:T(1,128)S(1)} collective-permute-done((f32[2,6,1,128]{3,2,1,0:T(1,128)S(1)}, f32[2,6,1,128]{3,2,1,0:T(1,128)S(1)}, u32[]{:S(2)}, u32[]{:S(2)}) %collective-permute-start.3) | collective-permute-done | bytes 6176 | tf_op jit(solution)/shard_map/ppermute | solution.py:24
  158.7 2.5 %collective-permute-done.5 = f32[2,1,4,128]{3,2,1,0:T(4,128)S(1)} collective-permute-done((f32[2,1,4,128]{3,2,1,0:T(4,128)S(1)}, f32[2,1,4,128]{3,2,1,0:T(4,128)S(1)}, u32[]{:S(2)}, u32[]{:S(2)}) %collective-permute-start.5) | collective-permute-done | bytes 4128 | tf_op jit(solution)/shard_map/ppermute | solution.py:24
  163.5 3.6 %collective-permute-start.7 = (f32[2,6,1,128]{3,2,1,0:T(1,128)S(1)}, f32[2,6,1,128]{3,2,1,0:T(1,128)S(1)}, u32[]{:S(2)}, u32[]{:S(2)}) collective-permute-start(f32[2,6,1,128]{3,2,1,0:T(1,128)S(1)} %get-tuple-element.16), channel_id=1, source_target_pairs={{0,1},{1,2},{2,3},{4,5},{5,6},{6,7},{8,9},{9,10},{10,11},{12,13},{... | collective-permute-start | bytes 18440 | tf_op jit(solution)/shard_map/ppermute | solution.py:24
  167.1 2.8 %collective-permute-done.7 = f32[2,6,1,128]{3,2,1,0:T(1,128)S(1)} collective-permute-done((f32[2,6,1,128]{3,2,1,0:T(1,128)S(1)}, f32[2,6,1,128]{3,2,1,0:T(1,128)S(1)}, u32[]{:S(2)}, u32[]{:S(2)}) %collective-permute-start.7) | collective-permute-done | bytes 6176 | tf_op jit(solution)/shard_map/ppermute | solution.py:24
  174.3 2.5 %collective-permute-done.9 = f32[2,1,4,128]{3,2,1,0:T(4,128)S(1)} collective-permute-done((f32[2,1,4,128]{3,2,1,0:T(4,128)S(1)}, f32[2,1,4,128]{3,2,1,0:T(4,128)S(1)}, u32[]{:S(2)}, u32[]{:S(2)}) %collective-permute-start.9) | collective-permute-done | bytes 4128 | tf_op jit(solution)/shard_map/ppermute | solution.py:24
  178.8 3.9 %collective-permute-start.11 = (f32[2,6,1,128]{3,2,1,0:T(1,128)S(1)}, f32[2,6,1,128]{3,2,1,0:T(1,128)S(1)}, u32[]{:S(2)}, u32[]{:S(2)}) collective-permute-start(f32[2,6,1,128]{3,2,1,0:T(1,128)S(1)} %get-tuple-element.14), channel_id=1, source_target_pairs={{0,1},{1,2},{2,3},{4,5},{5,6},{6,7},{8,9},{9,10},{10,11},{12,13},{... | collective-permute-start | bytes 18440 | tf_op jit(solution)/shard_map/ppermute | solution.py:24
  189.7 2.5 %collective-permute-done.13 = f32[2,1,4,128]{3,2,1,0:T(4,128)S(1)} collective-permute-done((f32[2,1,4,128]{3,2,1,0:T(4,128)S(1)}, f32[2,1,4,128]{3,2,1,0:T(4,128)S(1)}, u32[]{:S(2)}, u32[]{:S(2)}) %collective-permute-start.13) | collective-permute-done | bytes 4128 | tf_op jit(solution)/shard_map/ppermute | solution.py:24
  194.1 3.9 %collective-permute-start.15 = (f32[2,6,1,128]{3,2,1,0:T(1,128)S(1)}, f32[2,6,1,128]{3,2,1,0:T(1,128)S(1)}, u32[]{:S(2)}, u32[]{:S(2)}) collective-permute-start(f32[2,6,1,128]{3,2,1,0:T(1,128)S(1)} %get-tuple-element.12), channel_id=1, source_target_pairs={{0,1},{1,2},{2,3},{4,5},{5,6},{6,7},{8,9},{9,10},{10,11},{12,13},{... | collective-permute-start | bytes 18440 | tf_op jit(solution)/shard_map/ppermute | solution.py:24
  (86 shorter events, 39.3 us)
Async XLA Ops:
  6.5 21.7 %copy-start = (bf16[1,1,32,8,2048]{4,3,2,1,0:T(8,128)(2,1)S(1)}, bf16[1,1,32,8,2048]{4,3,2,1,0:T(8,128)(2,1)}, u32[]{:S(2)}) copy-start(bf16[1,1,32,8,2048]{4,3,2,1,0:T(8,128)(2,1)} %param.9) | copy-start | bytes 3145732
  6.5 81.0 %reduce-scatter.4.cloned.1.call-start = ((), (), s32[]{:S(2)}) async-start(), calls=%async_computation.3 | async-start | bytes 5242880
  23.0 5.2 %copy-start.1 = (bf16[1,1,32,8,2048]{4,3,2,1,0:T(8,128)(2,1)S(1)}, bf16[1,1,32,8,2048]{4,3,2,1,0:T(8,128)(2,1)}, u32[]{:S(2)}) copy-start(bf16[1,1,32,8,2048]{4,3,2,1,0:T(8,128)(2,1)} %param.10) | copy-start | bytes 3145732
  33.7 10.9 %copy-start.4 = (s32[2]{0:T(128)S(1)}, s32[2]{0:T(128)}, u32[]{:S(2)}) copy-start(s32[2]{0:T(128)} %constant.93) | copy-start | bytes 28
  33.7 11.0 %copy-start.5 = (s32[2]{0:T(128)S(1)}, s32[2]{0:T(128)}, u32[]{:S(2)}) copy-start(s32[2]{0:T(128)} %constant.96) | copy-start | bytes 28
  53.4 44.7 %all-to-all-start = ((s32[1,32,128]{2,0,1:T(1,128)}), s32[1,32,128]{2,0,1:T(1,128)S(1)}, u32[]{:S(2)}, u32[]{:S(2)}) async-start(s32[1,32,128]{2,0,1:T(1,128)} %bitcast.7), calls=%async_computation | async-start | bytes 32768 | tf_op jit(solution)/shard_map/all_to_all | solution.py:94
  98.1 10.0 %all-to-all-start.1 = ((f32[2,32,128]{2,0,1:T(2,128)}), f32[2,32,128]{2,0,1:T(2,128)S(1)}, u32[]{:S(2)}, u32[]{:S(2)}) async-start(f32[2,32,128]{2,0,1:T(2,128)} %copy.43), calls=%async_computation.1 | async-start | bytes 65536 | tf_op jit(solution)/shard_map/all_to_all | solution.py:93
  110.2 40.2 %copy-start.2 = (f32[4,4,128]{2,1,0:T(4,128)S(1)}, f32[4,4,128]{2,1,0:T(4,128)}, u32[]{:S(2)}) copy-start(f32[4,4,128]{2,1,0:T(4,128)} %param.15) | copy-start | bytes 24580
  136.6 4.9 %collective-permute-start = (f32[2,1,4,128]{3,2,1,0:T(4,128)S(1)}, f32[2,1,4,128]{3,2,1,0:T(4,128)S(1)}, u32[]{:S(2)}, u32[]{:S(2)}) collective-permute-start(f32[2,1,4,128]{3,2,1,0:T(4,128)S(1)} %get-tuple-element.26), channel_id=1, source_target_pairs={{4,0},{8,4},{12,8},{16,12},{20,16},{24,20},{28,24},{5,1},{9,5},{13... | collective-permute-start | bytes 12296 | tf_op jit(solution)/shard_map/ppermute | solution.py:26
  139.5 4.9 %collective-permute-start.1 = (f32[2,1,4,128]{3,2,1,0:T(4,128)S(1)}, f32[2,1,4,128]{3,2,1,0:T(4,128)S(1)}, u32[]{:S(2)}, u32[]{:S(2)}) collective-permute-start(f32[2,1,4,128]{3,2,1,0:T(4,128)S(1)} %get-tuple-element.25), channel_id=1, source_target_pairs={{0,4},{4,8},{8,12},{12,16},{16,20},{20,24},{24,28},{1,5},{5,9},{9,... | collective-permute-start | bytes 12296 | tf_op jit(solution)/shard_map/ppermute | solution.py:24
  144.5 5.9 %collective-permute-start.2 = (f32[2,6,1,128]{3,2,1,0:T(1,128)S(1)}, f32[2,6,1,128]{3,2,1,0:T(1,128)S(1)}, u32[]{:S(2)}, u32[]{:S(2)}) collective-permute-start(f32[2,6,1,128]{3,2,1,0:T(1,128)S(1)} %get-tuple-element.17), channel_id=1, source_target_pairs={{1,0},{2,1},{3,2},{5,4},{6,5},{7,6},{9,8},{10,9},{11,10},{13,12},{... | collective-permute-start | bytes 18440 | tf_op jit(solution)/shard_map/ppermute | solution.py:26
  147.8 6.4 %collective-permute-start.3 = (f32[2,6,1,128]{3,2,1,0:T(1,128)S(1)}, f32[2,6,1,128]{3,2,1,0:T(1,128)S(1)}, u32[]{:S(2)}, u32[]{:S(2)}) collective-permute-start(f32[2,6,1,128]{3,2,1,0:T(1,128)S(1)} %get-tuple-element.18), channel_id=1, source_target_pairs={{0,1},{1,2},{2,3},{4,5},{5,6},{6,7},{8,9},{9,10},{10,11},{12,13},{... | collective-permute-start | bytes 18440 | tf_op jit(solution)/shard_map/ppermute | solution.py:24
  154.4 4.3 %collective-permute-start.4 = (f32[2,1,4,128]{3,2,1,0:T(4,128)S(1)}, f32[2,1,4,128]{3,2,1,0:T(4,128)S(1)}, u32[]{:S(2)}, u32[]{:S(2)}) collective-permute-start(f32[2,1,4,128]{3,2,1,0:T(4,128)S(1)} %get-tuple-element.24), channel_id=1, source_target_pairs={{4,0},{8,4},{12,8},{16,12},{20,16},{24,20},{28,24},{5,1},{9,5},{13... | collective-permute-start | bytes 12296 | tf_op jit(solution)/shard_map/ppermute | solution.py:26
  156.3 4.9 %collective-permute-start.5 = (f32[2,1,4,128]{3,2,1,0:T(4,128)S(1)}, f32[2,1,4,128]{3,2,1,0:T(4,128)S(1)}, u32[]{:S(2)}, u32[]{:S(2)}) collective-permute-start(f32[2,1,4,128]{3,2,1,0:T(4,128)S(1)} %get-tuple-element.23), channel_id=1, source_target_pairs={{0,4},{4,8},{8,12},{12,16},{16,20},{20,24},{24,28},{1,5},{5,9},{9,... | collective-permute-start | bytes 12296 | tf_op jit(solution)/shard_map/ppermute | solution.py:24
  161.2 5.9 %collective-permute-start.6 = (f32[2,6,1,128]{3,2,1,0:T(1,128)S(1)}, f32[2,6,1,128]{3,2,1,0:T(1,128)S(1)}, u32[]{:S(2)}, u32[]{:S(2)}) collective-permute-start(f32[2,6,1,128]{3,2,1,0:T(1,128)S(1)} %get-tuple-element.15), channel_id=1, source_target_pairs={{1,0},{2,1},{3,2},{5,4},{6,5},{7,6},{9,8},{10,9},{11,10},{13,12},{... | collective-permute-start | bytes 18440 | tf_op jit(solution)/shard_map/ppermute | solution.py:26
  163.5 6.4 %collective-permute-start.7 = (f32[2,6,1,128]{3,2,1,0:T(1,128)S(1)}, f32[2,6,1,128]{3,2,1,0:T(1,128)S(1)}, u32[]{:S(2)}, u32[]{:S(2)}) collective-permute-start(f32[2,6,1,128]{3,2,1,0:T(1,128)S(1)} %get-tuple-element.16), channel_id=1, source_target_pairs={{0,1},{1,2},{2,3},{4,5},{5,6},{6,7},{8,9},{9,10},{10,11},{12,13},{... | collective-permute-start | bytes 18440 | tf_op jit(solution)/shard_map/ppermute | solution.py:24
  170.0 4.3 %collective-permute-start.8 = (f32[2,1,4,128]{3,2,1,0:T(4,128)S(1)}, f32[2,1,4,128]{3,2,1,0:T(4,128)S(1)}, u32[]{:S(2)}, u32[]{:S(2)}) collective-permute-start(f32[2,1,4,128]{3,2,1,0:T(4,128)S(1)} %get-tuple-element.22), channel_id=1, source_target_pairs={{4,0},{8,4},{12,8},{16,12},{20,16},{24,20},{28,24},{5,1},{9,5},{13... | collective-permute-start | bytes 12296 | tf_op jit(solution)/shard_map/ppermute | solution.py:26
  171.9 4.9 %collective-permute-start.9 = (f32[2,1,4,128]{3,2,1,0:T(4,128)S(1)}, f32[2,1,4,128]{3,2,1,0:T(4,128)S(1)}, u32[]{:S(2)}, u32[]{:S(2)}) collective-permute-start(f32[2,1,4,128]{3,2,1,0:T(4,128)S(1)} %get-tuple-element.21), channel_id=1, source_target_pairs={{0,4},{4,8},{8,12},{12,16},{16,20},{20,24},{24,28},{1,5},{5,9},{9,... | collective-permute-start | bytes 12296 | tf_op jit(solution)/shard_map/ppermute | solution.py:24
  176.8 5.9 %collective-permute-start.10 = (f32[2,6,1,128]{3,2,1,0:T(1,128)S(1)}, f32[2,6,1,128]{3,2,1,0:T(1,128)S(1)}, u32[]{:S(2)}, u32[]{:S(2)}) collective-permute-start(f32[2,6,1,128]{3,2,1,0:T(1,128)S(1)} %get-tuple-element.13), channel_id=1, source_target_pairs={{1,0},{2,1},{3,2},{5,4},{6,5},{7,6},{9,8},{10,9},{11,10},{13,12},{... | collective-permute-start | bytes 18440 | tf_op jit(solution)/shard_map/ppermute | solution.py:26
  178.8 6.4 %collective-permute-start.11 = (f32[2,6,1,128]{3,2,1,0:T(1,128)S(1)}, f32[2,6,1,128]{3,2,1,0:T(1,128)S(1)}, u32[]{:S(2)}, u32[]{:S(2)}) collective-permute-start(f32[2,6,1,128]{3,2,1,0:T(1,128)S(1)} %get-tuple-element.14), channel_id=1, source_target_pairs={{0,1},{1,2},{2,3},{4,5},{5,6},{6,7},{8,9},{9,10},{10,11},{12,13},{... | collective-permute-start | bytes 18440 | tf_op jit(solution)/shard_map/ppermute | solution.py:24
  185.3 4.3 %collective-permute-start.12 = (f32[2,1,4,128]{3,2,1,0:T(4,128)S(1)}, f32[2,1,4,128]{3,2,1,0:T(4,128)S(1)}, u32[]{:S(2)}, u32[]{:S(2)}) collective-permute-start(f32[2,1,4,128]{3,2,1,0:T(4,128)S(1)} %get-tuple-element.20), channel_id=1, source_target_pairs={{4,0},{8,4},{12,8},{16,12},{20,16},{24,20},{28,24},{5,1},{9,5},{13... | collective-permute-start | bytes 12296 | tf_op jit(solution)/shard_map/ppermute | solution.py:26
  187.2 4.9 %collective-permute-start.13 = (f32[2,1,4,128]{3,2,1,0:T(4,128)S(1)}, f32[2,1,4,128]{3,2,1,0:T(4,128)S(1)}, u32[]{:S(2)}, u32[]{:S(2)}) collective-permute-start(f32[2,1,4,128]{3,2,1,0:T(4,128)S(1)} %get-tuple-element.19), channel_id=1, source_target_pairs={{0,4},{4,8},{8,12},{12,16},{16,20},{20,24},{24,28},{1,5},{5,9},{9,... | collective-permute-start | bytes 12296 | tf_op jit(solution)/shard_map/ppermute | solution.py:24
  192.2 5.9 %collective-permute-start.14 = (f32[2,6,1,128]{3,2,1,0:T(1,128)S(1)}, f32[2,6,1,128]{3,2,1,0:T(1,128)S(1)}, u32[]{:S(2)}, u32[]{:S(2)}) collective-permute-start(f32[2,6,1,128]{3,2,1,0:T(1,128)S(1)} %get-tuple-element.11), channel_id=1, source_target_pairs={{1,0},{2,1},{3,2},{5,4},{6,5},{7,6},{9,8},{10,9},{11,10},{13,12},{... | collective-permute-start | bytes 18440 | tf_op jit(solution)/shard_map/ppermute | solution.py:26
  194.1 6.4 %collective-permute-start.15 = (f32[2,6,1,128]{3,2,1,0:T(1,128)S(1)}, f32[2,6,1,128]{3,2,1,0:T(1,128)S(1)}, u32[]{:S(2)}, u32[]{:S(2)}) collective-permute-start(f32[2,6,1,128]{3,2,1,0:T(1,128)S(1)} %get-tuple-element.12), channel_id=1, source_target_pairs={{0,1},{1,2},{2,3},{4,5},{5,6},{6,7},{8,9},{9,10},{10,11},{12,13},{... | collective-permute-start | bytes 18440 | tf_op jit(solution)/shard_map/ppermute | solution.py:24
  (2 other events, 5.1 us)
Sparse Core Ops, SparseCore 0:
  33.8 53.6 reduce-scatter.3
where the time goes:
time: 209 us; the launch traced here: 208 us
  waiting for transfers between devices  55.6 us (27%)
  starting transfers between devices  51.9 us (25%)
  other arithmetic  38.9 us (19%)
  local copies, waits for them, and re-layouts  26.9 us (13%)
  blocking collectives  14.4 us (7%)
  between operations  13.8 us (7%)
  matrix products  6.52 us (3%)
    unnamed x2, waiting for transfers between devices  28.3 us
    scatter-add x1, other arithmetic, per_device(): jnp.zeros((NVEC, points + 1), jnp.float32).at[:, received_places[0]]  26 us
    ppermute x8, starting transfers between devices, extended(): lax.ppermute(tail, axis, [(i, (i + 1) % count) for i in range(ends)])  23.1 us
    ppermute x8, waiting for transfers between devices, extended(): lax.ppermute(tail, axis, [(i, (i + 1) % count) for i in range(ends)])  22.2 us
    ppermute x8, starting transfers between devices, extended(): lax.ppermute(head, axis, [((i + 1) % count, i) for i in range(ends)])  18.2 us
    all_gather x1, blocking collectives, per_device(): gathered = lax.all_gather(vectors, 'row', axis=2, tiled=True)  14.4 us
    unnamed x20, local copies, waits for them, and re-layouts  14.2 us
    another operation x2, other arithmetic  9.25 us
  transfers between devices with their start and end apart: 19, of which 10 were waited for; matrix products, arithmetic and copies ran while one was open for 14% of the time, Pallas kernels for 0%

commit v1 on v0

v1 whole, which is shorter than its diff:
```python
import functools

import jax
import jax.numpy as jnp
from jax import lax
from jax.experimental import pallas as pl
from jax.experimental.pallas import tpu as pltpu
from jax.sharding import PartitionSpec as P

CX = 4
CY = 4
TILE_ROWS = 4
TILE_COLS = 8
LANES = 128
MESH = pl.DeviceIdType.MESH
F32 = jnp.float32
BF16 = jnp.bfloat16
NT = (((1,), (1,)), ((), ()))
SIDES = [(a, b) for a in (-1, 0, 1) for b in (-1, 0, 1) if (a, b) != (0, 0)]


def dot_nt(a, b):
    return lax.dot_general(a, b, NT, preferred_element_type=F32)


def pieces(x):
    first = x.astype(BF16).astype(F32)
    rest = x - first
    second = rest.astype(BF16).astype(F32)
    return first, second, rest - second


def iota(shape, dim):
    return lax.broadcasted_iota(jnp.int32, shape, dim)


def kernel(
    rows, cols, kmax, leaf,
    x_ref, right_hbm, left_hbm, rank_ref, leaf_hbm, places_ref, perm_ref, kappa_ref,
    out_ref,
    right_ref, left_ref, leaf_ref, xg, x32, part, rs, slot_hot,
    msend, rm, vsend, rv, lane_hot, brick, hb, kb, ext, coef, scale,
    local_sem, ag_sem, m_sem, rs_sem, v_sem, k_send, k_recv, h_send, h_recv,
):
    nvec, points = x_ref.shape
    tile = right_ref.shape[1]
    taps = right_ref.shape[0]
    devices = rows * cols
    nleaf = leaf_ref.shape[0]
    cells = CX * CY
    blocks = points // LANES
    r = lax.axis_index("row")
    c = lax.axis_index("col")
    me = r * cols + c

    loads = [
        pltpu.make_async_copy(right_hbm, right_ref, local_sem.at[0]),
        pltpu.make_async_copy(left_hbm, left_ref, local_sem.at[1]),
        pltpu.make_async_copy(leaf_hbm, leaf_ref, local_sem.at[2]),
    ]
    for load in loads:
        load.start()

    def at(flat):
        return {"row": flat // cols, "col": flat % cols}

    barrier = pltpu.get_barrier_semaphore()

    def greet(k, carry):
        pl.semaphore_signal(
            barrier, inc=1, device_id=at(lax.rem(me + k, devices)), device_id_type=MESH
        )
        return carry

    lax.fori_loop(1, devices, greet, 0)

    targets = perm_ref[pl.ds(pl.multiple_of(c * blocks, 8), blocks), :]
    dev_of = targets // points
    place = targets % points
    place_hi = (place // LANES).astype(F32)
    place_lo = (place % LANES).astype(F32)
    dev_ids = iota((devices, LANES), 0)
    hots = [(dev_of[b : b + 1, :] == dev_ids).astype(F32) for b in range(blocks)]
    before = (iota((LANES, LANES), 0) < iota((LANES, LANES), 1)).astype(BF16)
    all_hot = jnp.concatenate(hots, axis=0).astype(BF16)
    inside = jnp.dot(all_hot, before, preferred_element_type=F32)
    totals = jnp.dot(all_hot, jnp.ones((LANES, LANES), BF16), preferred_element_type=F32)
    offset = jnp.zeros((devices, LANES), F32)
    lane_rows = iota((LANES, LANES), 0).astype(F32)
    for b in range(blocks):
        span = slice(b * devices, (b + 1) * devices)
        rank = jnp.sum(hots[b] * (inside[span] + offset), axis=0, keepdims=True)
        offset = offset + totals[span]
        slot_hot[:, b * LANES : (b + 1) * LANES] = (rank == lane_rows).astype(BF16)
    meta = jnp.concatenate(
        [
            jnp.concatenate(
                [hots[b] * place_hi[b : b + 1, :], hots[b] * place_lo[b : b + 1, :]], axis=0
            ).astype(BF16)
            for b in range(blocks)
        ],
        axis=1,
    )
    meta = dot_nt(meta, slot_hot[...])
    for h in range(2):
        msend[:, h, :] = meta[h * devices : (h + 1) * devices]

    xg[r] = x_ref[...]
    ext[...] = jnp.zeros_like(ext)
    coef[...] = jnp.zeros_like(coef)
    scale[...] = jnp.zeros_like(scale)
    pl.semaphore_wait(barrier, devices - 1)

    def spread(k, carry):
        pltpu.make_async_remote_copy(
            src_ref=x_ref, dst_ref=xg.at[r], send_sem=ag_sem.at[0], recv_sem=ag_sem.at[1],
            device_id={"row": lax.rem(r + k, rows), "col": c}, device_id_type=MESH,
        ).start()
        return carry

    lax.fori_loop(1, rows, spread, 0)

    def exchange(src, dst, sem):
        def send(k, carry):
            to = lax.rem(me + k, devices)
            pltpu.make_async_remote_copy(
                src_ref=src.at[to], dst_ref=dst.at[k - 1], send_sem=sem.at[0],
                recv_sem=sem.at[1], device_id=at(to), device_id_type=MESH,
            ).start()
            return carry

        lax.fori_loop(1, devices, send, 0)
        dst[devices - 1] = src[me]

    def settle(ref, count, sem):
        done = ref.at[pl.ds(0, count)]
        copy = pltpu.make_async_remote_copy(
            src_ref=done, dst_ref=done, send_sem=sem.at[0], recv_sem=sem.at[1],
            device_id=at(lax.rem(me + 1, devices)), device_id_type=MESH,
        )
        return copy

    def side(n):
        dr, dc = SIDES[n]
        rr, cc = r + dr, c + dc
        ok = (rr >= 0) & (rr < rows) & (cc >= 0) & (cc < cols)
        return ok, {"row": jnp.clip(rr, 0, rows - 1), "col": jnp.clip(cc, 0, cols - 1)}

    def side_copy(src, dst, send, recv, n, incoming):
        slot = n if incoming else len(SIDES) - 1 - n
        return pltpu.make_async_remote_copy(
            src_ref=src, dst_ref=dst.at[slot], send_sem=send.at[n], recv_sem=recv.at[slot],
            device_id=side(n)[1], device_id_type=MESH,
        )

    def sides_start(src, dst, send, recv):
        for n in range(len(SIDES)):
            @pl.when(side(n)[0])
            def _():
                side_copy(src, dst, send, recv, n, False).start()

    def sides_wait(src, dst, send, recv):
        for n in range(len(SIDES)):
            @pl.when(side(n)[0])
            def _():
                side_copy(src, dst, send, recv, n, True).wait_recv()
                side_copy(src, dst, send, recv, n, False).wait_send()

    exchange(msend, rm, m_sem)
    sides_start(kappa_ref, kb, k_send, k_recv)

    gathered = settle(xg, rows - 1, ag_sem)
    gathered.wait_recv()
    per = tile // points
    for s in range(rows):
        b, j = s // per, s % per
        x32[nvec * b : nvec * (b + 1), j * points : (j + 1) * points] = xg[s].astype(F32)
    loads[0].wait()
    wide = TILE_COLS * nvec
    projected = dot_nt(x32[...].astype(BF16), right_ref[...])
    lane = iota((1, taps), 1)
    lane_tile, lane_k = lane // kmax, lane % kmax
    ranks = jnp.zeros((1, taps), jnp.int32)
    for t in range(TILE_ROWS * TILE_COLS):
        ranks = jnp.where(lane_tile == t, rank_ref[t], ranks)
    keep = (lane_tile % TILE_COLS == iota((wide, taps), 0) // nvec) & (lane_k < ranks)
    projected = jnp.where(keep, projected, 0.0).astype(BF16)
    tall = TILE_ROWS * nvec
    fold = (iota((tall, wide), 0) % nvec == iota((tall, wide), 1) % nvec).astype(BF16)
    spread_out = jnp.dot(fold, projected, preferred_element_type=F32)
    own_row = lane_tile // TILE_COLS == iota((tall, taps), 0) // nvec
    spread_out = jnp.where(own_row, spread_out, 0.0).astype(BF16)
    loads[1].wait()
    far = jnp.dot(spread_out, left_ref[...], preferred_element_type=F32)
    loads[2].wait()
    subs = points // leaf
    near = []
    for l in range(nleaf):
        column = places_ref[2 * l + 1]
        held = xg[column // subs].astype(F32)
        sub = column % subs
        pick = jnp.zeros((nvec, leaf), F32)
        for q in range(subs):
            pick += jnp.where(sub == q, 1.0, 0.0) * held[:, q * leaf : (q + 1) * leaf]
        near.append(dot_nt(pick.astype(BF16), leaf_ref[l]))
    for d in range(cols):
        a, start = d * points // tile, d * points % tile
        for q in range(subs):
            total = far[nvec * a : nvec * (a + 1), start + q * leaf : start + (q + 1) * leaf]
            for l in range(nleaf):
                total += jnp.where(places_ref[2 * l] == d * subs + q, 1.0, 0.0) * near[l]
            part[d, :, q * leaf : (q + 1) * leaf] = total

    def share(k, carry):
        to = lax.rem(c + k, cols)
        pltpu.make_async_remote_copy(
            src_ref=part.at[to], dst_ref=rs.at[k - 1], send_sem=rs_sem.at[0],
            recv_sem=rs_sem.at[1], device_id={"row": r, "col": to}, device_id_type=MESH,
        ).start()
        return carry

    lax.fori_loop(1, cols, share, 0)

    sides_wait(kappa_ref, kb, k_send, k_recv)
    strip = 4 * CY

    def laid(ref, get, every):
        for n, (dr, dc) in enumerate(every):
            value = get(dr, dc)
            for x in range(CX):
                at_row = ((dr + 1) * CX + x) * strip + (dc + 1) * CY
                ref[at_row : at_row + CY, :] = value[x * CY : (x + 1) * CY, :]

    every = SIDES + [(0, 0)]

    def valid(dr, dc):
        return (r + dr >= 0) & (r + dr < rows) & (c + dc >= 0) & (c + dc < cols)

    def stiffness(dr, dc):
        if (dr, dc) == (0, 0):
            return (6.0 + kappa_ref[...]) * 0.125
        return jnp.where(valid(dr, dc), (6.0 + kb[SIDES.index((dr, dc))]) * 0.125, 0.0)

    laid(coef, stiffness, every)
    laid(
        scale,
        lambda dr, dc: jnp.full((cells, LANES), jnp.where(valid(dr, dc), 0.125, 0.0), F32),
        every,
    )
    metas = settle(rm, devices - 1, m_sem)
    metas.wait_recv()
    for s in range(devices):
        lane_hot[:, s * LANES : (s + 1) * LANES] = (rm[s, 1:2, :] == lane_rows).astype(BF16)

    shares = settle(rs, cols - 1, rs_sem)
    shares.wait_recv()
    action = part[c]
    for k in range(cols - 1):
        action += rs[k]

    terms = pieces(action)
    left_side = jnp.concatenate(
        [
            jnp.concatenate(
                [
                    jnp.where(
                        dev_of[b : b + 1, :] == dev_ids,
                        term[v : v + 1, b * LANES : (b + 1) * LANES],
                        0.0,
                    )
                    for term in terms
                    for v in range(nvec)
                ],
                axis=0,
            ).astype(BF16)
            for b in range(blocks)
        ],
        axis=1,
    )
    packed = dot_nt(left_side, slot_hot[...])
    size = nvec * devices
    packed = packed[:size] + packed[size : 2 * size] + packed[2 * size :]
    for v in range(nvec):
        vsend[:, v, :] = packed[v * devices : (v + 1) * devices]
    exchange(vsend, rv, v_sem)
    values = settle(rv, devices - 1, v_sem)
    values.wait_recv()

    cell_rows = iota((cells, LANES), 0).astype(F32)
    placed = []
    for s in range(devices):
        hit = rm[s, 0:1, :] == cell_rows
        bits = pieces(rv[s])
        placed.append(
            jnp.concatenate(
                [jnp.where(hit, bit[v : v + 1, :], 0.0) for bit in bits for v in range(nvec)],
                axis=0,
            ).astype(BF16)
        )
    field = dot_nt(jnp.concatenate(placed, axis=1), lane_hot[...])
    size = nvec * cells
    field = field[:size] + field[size : 2 * size] + field[2 * size :]
    for v in range(nvec):
        brick[v] = field[v * cells : (v + 1) * cells]
    sides_start(brick, hb, h_send, h_recv)
    gathered.wait_send()
    metas.wait_send()
    shares.wait_send()
    values.wait_send()
    sides_wait(brick, hb, h_send, h_recv)

    def bricks(v, dr, dc):
        if (dr, dc) == (0, 0):
            return brick[v]
        return jnp.where(valid(dr, dc), hb[SIDES.index((dr, dc)), v], 0.0)

    for v in range(nvec):
        laid(ext.at[v], functools.partial(bricks, v), every)
        cur = ext[v]
        for step in range(4):
            mid = cur[strip:-strip]
            z = iota(mid.shape, 1)
            beside = cur[2 * strip :] + cur[: -2 * strip]
            beside += pltpu.roll(mid, 1, 0) + pltpu.roll(mid, mid.shape[0] - 1, 0)
            beside += jnp.where(z > 0, pltpu.roll(mid, 1, 1), 0.0)
            beside += jnp.where(z < LANES - 1, pltpu.roll(mid, LANES - 1, 1), 0.0)
            low = (step + 1) * strip
            span = slice(low, ext.shape[1] - low)
            cur = coef[span, :] * mid - scale[span, :] * beside
        for x in range(CX):
            out_ref[v, x * CY : (x + 1) * CY, :] = cur[x * strip + CY : x * strip + 2 * CY]


def per_device(
    vectors, lr_left, lr_right, tile_rank, leaf_values, leaf_places, cluster_perm, kappa
):
    rows, cols = lax.axis_size("row"), lax.axis_size("col")
    devices = rows * cols
    nvec, _, points = vectors.shape
    tiles, kmax, tile = lr_left.shape[2:]
    nleaf, leaf = leaf_values.shape[2:4]
    cells, lanes = CX * CY, kappa.shape[2]
    taps = tiles * kmax
    strip, deep = 4 * CY, 3 * CX * 4 * CY
    vmem = pl.BlockSpec(memory_space=pltpu.VMEM)
    smem = pl.BlockSpec(memory_space=pltpu.SMEM)
    hbm = pl.BlockSpec(memory_space=pl.ANY)
    dma = pltpu.SemaphoreType.DMA
    out = pl.pallas_call(
        functools.partial(kernel, rows, cols, kmax, leaf),
        out_shape=jax.ShapeDtypeStruct((nvec, cells, lanes), F32),
        in_specs=[vmem, hbm, hbm, smem, hbm, smem, vmem, vmem],
        out_specs=vmem,
        scratch_shapes=[
            pltpu.VMEM((taps, tile), BF16),
            pltpu.VMEM((taps, tile), BF16),
            pltpu.VMEM((nleaf, leaf, leaf), BF16),
            pltpu.VMEM((rows, nvec, points), BF16),
            pltpu.VMEM((TILE_COLS * nvec, tile), F32),
            pltpu.VMEM((cols, nvec, points), F32),
            pltpu.VMEM((cols - 1, nvec, points), F32),
            pltpu.VMEM((LANES, points), BF16),
            pltpu.VMEM((devices, 2, LANES), F32),
            pltpu.VMEM((devices, 2, LANES), F32),
            pltpu.VMEM((devices, nvec, LANES), F32),
            pltpu.VMEM((devices, nvec, LANES), F32),
            pltpu.VMEM((LANES, devices * LANES), BF16),
            pltpu.VMEM((nvec, cells, lanes), F32),
            pltpu.VMEM((len(SIDES), nvec, cells, lanes), F32),
            pltpu.VMEM((len(SIDES), cells, lanes), F32),
            pltpu.VMEM((nvec, deep, lanes), F32),
            pltpu.VMEM((deep, lanes), F32),
            pltpu.VMEM((deep, lanes), F32),
            dma((3,)), dma((2,)), dma((2,)), dma((2,)), dma((2,)),
            dma((len(SIDES),)), dma((len(SIDES),)), dma((len(SIDES),)), dma((len(SIDES),)),
        ],
        compiler_params=pltpu.CompilerParams(collective_id=0, has_side_effects=True),
    )(
        vectors.reshape(nvec, points),
        lr_right.reshape(taps, tile),
        lr_left.reshape(taps, tile),
        tile_rank.reshape(tiles),
        leaf_values.reshape(nleaf, leaf, leaf),
        leaf_places.reshape(2 * nleaf),
        cluster_perm.reshape(-1, LANES),
        kappa.reshape(cells, lanes),
    )
    return out.reshape(nvec, CX, CY, lanes)


def solution(mesh):
    in_specs = (
        P(None, "col", "row"),
        P("row", "col", None, None, None),
        P("row", "col", None, None, None),
        P("row", "col", None),
        P("row", "col", None, None, None),
        P("row", "col", None, None),
        P("row", None),
        P("row", "col", None),
    )
    out_specs = P(None, "row", "col", None)
    return jax.shard_map(
        per_device, mesh=mesh, in_specs=in_specs, out_specs=out_specs, check_vma=False
    )
```

time: 209 us -> 30.7 us (0.15)
  the two profiles are of different devices: /device:TPU:12 before, /device:TPU:0 now
where the time goes in v1:
time: 30.7 us; the launch traced here: 30.4 us
  Pallas kernels  27.7 us (90%)
  local copies, waits for them, and re-layouts  2.67 us (9%)
    pallas_call x1, Pallas kernels, per_device(): pl.pallas_call(functools.partial(kernel, rows, cols, kmax, leaf), out_sha...  27.7 us
    unnamed x2, local copies, waits for them, and re-layouts  2.08 us

profile of v1, /device:TPU:0, one launch (start us, length us, event | category | flops | bytes accessed | tf_op | source)
XLA Modules:
  0.0 30.4 jit_solution(18155232033149688518)
XLA Ops:
  0.0 0.8 %copy.10 = s32[1,1,8,2]{3,2,1,0:T(8,128)S(1)} copy(s32[1,1,8,2]{2,3,1,0:T(2,128)} %param.13) | data formatting | bytes 128 | tf_op args[5]
  0.8 0.6 %reshape.32.places_ref = s32[16]{0:T(128)} reshape(s32[1,1,8,2]{3,2,1,0:T(8,128)S(1)} %copy.10) | data formatting | bytes 128 | tf_op jit(solution)/shard_map/reshape | solution.py:384
  1.3 27.7 %shard_map.82 = f32[2,16,128]{2,1,0:T(8,128)} custom-call(bf16[2,2048]{1,0:T(2,128)(2,1)} %bitcast.15, bf16[256,2048]{1,0:T(8,128)(2,1)} %bitcast.11, bf16[256,2048]{1,0:T(8,128)(2,1)} %bitcast.12, s32[32]{0:T(128)} %bitcast.17, bf16[8,512,512]{2,1,0:T(8,128)(2,1)} %bitcast.10, s32[16]{0:T(128)} %reshape.32.places_ref, s32[64,128]{1,0:T(8,128)} %bitcast.14, ...), custom_call_target="tpu_custom_call" | custom-call | tf_op jit(solution)/shard_map/pallas_call | solution.py:349
  29.1 1.3 %copy.12 = f32[2,4,4,128]{3,2,1,0:T(4,128)} copy(f32[2,4,4,128]{3,2,1,0:T(4,128)} %bitcast.13) | data formatting | bytes 32768

commit v2 on v1

--- a/solution.py
+++ b/solution.py
@@ -36,13 +36,13 @@
 
 def kernel(
     rows, cols, kmax, leaf,
-    x_ref, right_hbm, left_hbm, rank_ref, leaf_hbm, places_ref, perm_ref, kappa_ref,
+    x_hbm, right_hbm, left_hbm, rank_ref, leaf_hbm, places_ref, perm_hbm, kappa_hbm,
     out_ref,
-    right_ref, left_ref, leaf_ref, xg, x32, part, rs, slot_hot,
+    perm_ref, kappa_ref, right_ref, left_ref, leaf_ref, xg, x32, part, rs, slot_hot,
     msend, rm, vsend, rv, lane_hot, brick, hb, kb, ext, coef, scale,
     local_sem, ag_sem, m_sem, rs_sem, v_sem, k_send, k_recv, h_send, h_recv,
 ):
-    nvec, points = x_ref.shape
+    nvec, points = x_hbm.shape
     tile = right_ref.shape[1]
     taps = right_ref.shape[0]
     devices = rows * cols
@@ -53,28 +53,42 @@
     c = lax.axis_index("col")
     me = r * cols + c
 
+    own_x = pltpu.make_async_copy(x_hbm, xg.at[r], local_sem.at[3])
+    own_perm = pltpu.make_async_copy(
+        perm_hbm.at[pl.ds(pl.multiple_of(c * blocks, 8), blocks)], perm_ref, local_sem.at[4]
+    )
+    own_kappa = pltpu.make_async_copy(kappa_hbm, kappa_ref, local_sem.at[5])
     loads = [
         pltpu.make_async_copy(right_hbm, right_ref, local_sem.at[0]),
         pltpu.make_async_copy(left_hbm, left_ref, local_sem.at[1]),
         pltpu.make_async_copy(leaf_hbm, leaf_ref, local_sem.at[2]),
     ]
-    for load in loads:
+
+    def turned(place, by, count):
+        moved = place + by
+        return moved - jnp.where(moved >= count, count, 0)
+
+    barrier = pltpu.get_barrier_semaphore()
+    for k in range(1, rows):
+        pl.semaphore_signal(
+            barrier, inc=1, device_id={"row": turned(r, k, rows), "col": c}, device_id_type=MESH
+        )
+    for k in range(1, cols):
+        pl.semaphore_signal(
+            barrier, inc=1, device_id={"row": r, "col": turned(c, k, cols)}, device_id_type=MESH
+        )
+    for load in [own_x, own_perm, own_kappa] + loads:
         load.start()
-
-    def at(flat):
-        return {"row": flat // cols, "col": flat % cols}
-
-    barrier = pltpu.get_barrier_semaphore()
-
-    def greet(k, carry):
-        pl.semaphore_signal(
-            barrier, inc=1, device_id=at(lax.rem(me + k, devices)), device_id_type=MESH
-        )
-        return carry
-
-    lax.fori_loop(1, devices, greet, 0)
-
-    targets = perm_ref[pl.ds(pl.multiple_of(c * blocks, 8), blocks), :]
+    own_x.wait()
+    pl.semaphore_wait(barrier, rows + cols - 2)
+    for k in range(1, rows):
+        pltpu.make_async_remote_copy(
+            src_ref=xg.at[r], dst_ref=xg.at[r], send_sem=ag_sem.at[0], recv_sem=ag_sem.at[1],
+            device_id={"row": turned(r, k, rows), "col": c}, device_id_type=MESH,
+        ).start()
+
+    own_perm.wait()
+    targets = perm_ref[...]
     dev_of = targets // points
     place = targets % points
     place_hi = (place // LANES).astype(F32)
@@ -105,38 +119,27 @@
     for h in range(2):
         msend[:, h, :] = meta[h * devices : (h + 1) * devices]
 
-    xg[r] = x_ref[...]
     ext[...] = jnp.zeros_like(ext)
     coef[...] = jnp.zeros_like(coef)
     scale[...] = jnp.zeros_like(scale)
-    pl.semaphore_wait(barrier, devices - 1)
-
-    def spread(k, carry):
-        pltpu.make_async_remote_copy(
-            src_ref=x_ref, dst_ref=xg.at[r], send_sem=ag_sem.at[0], recv_sem=ag_sem.at[1],
-            device_id={"row": lax.rem(r + k, rows), "col": c}, device_id_type=MESH,
-        ).start()
-        return carry
-
-    lax.fori_loop(1, rows, spread, 0)
 
     def exchange(src, dst, sem):
-        def send(k, carry):
-            to = lax.rem(me + k, devices)
-            pltpu.make_async_remote_copy(
-                src_ref=src.at[to], dst_ref=dst.at[k - 1], send_sem=sem.at[0],
-                recv_sem=sem.at[1], device_id=at(to), device_id_type=MESH,
-            ).start()
-            return carry
-
-        lax.fori_loop(1, devices, send, 0)
+        for dr in range(rows):
+            for dc in range(cols):
+                if dr + dc:
+                    rr, cc = turned(r, dr, rows), turned(c, dc, cols)
+                    pltpu.make_async_remote_copy(
+                        src_ref=src.at[rr * cols + cc], dst_ref=dst.at[dr * cols + dc - 1],
+                        send_sem=sem.at[0], recv_sem=sem.at[1],
+                        device_id={"row": rr, "col": cc}, device_id_type=MESH,
+                    ).start()
         dst[devices - 1] = src[me]
 
     def settle(ref, count, sem):
         done = ref.at[pl.ds(0, count)]
         copy = pltpu.make_async_remote_copy(
             src_ref=done, dst_ref=done, send_sem=sem.at[0], recv_sem=sem.at[1],
-            device_id=at(lax.rem(me + 1, devices)), device_id_type=MESH,
+            device_id={"row": turned(r, 1, rows), "col": c}, device_id_type=MESH,
         )
         return copy
 
@@ -165,9 +168,6 @@
             def _():
                 side_copy(src, dst, send, recv, n, True).wait_recv()
                 side_copy(src, dst, send, recv, n, False).wait_send()
-
-    exchange(msend, rm, m_sem)
-    sides_start(kappa_ref, kb, k_send, k_recv)
 
     gathered = settle(xg, rows - 1, ag_sem)
     gathered.wait_recv()
@@ -196,7 +196,7 @@
     subs = points // leaf
     near = []
     for l in range(nleaf):
-        column = places_ref[2 * l + 1]
+        column = places_ref[1, l]
         held = xg[column // subs].astype(F32)
         sub = column % subs
         pick = jnp.zeros((nvec, leaf), F32)
@@ -208,49 +208,18 @@
         for q in range(subs):
             total = far[nvec * a : nvec * (a + 1), start + q * leaf : start + (q + 1) * leaf]
             for l in range(nleaf):
-                total += jnp.where(places_ref[2 * l] == d * subs + q, 1.0, 0.0) * near[l]
+                total += jnp.where(places_ref[0, l] == d * subs + q, 1.0, 0.0) * near[l]
             part[d, :, q * leaf : (q + 1) * leaf] = total
 
-    def share(k, carry):
-        to = lax.rem(c + k, cols)
+    for k in range(1, cols):
+        to = turned(c, k, cols)
         pltpu.make_async_remote_copy(
             src_ref=part.at[to], dst_ref=rs.at[k - 1], send_sem=rs_sem.at[0],
             recv_sem=rs_sem.at[1], device_id={"row": r, "col": to}, device_id_type=MESH,
         ).start()
-        return carry
-
-    lax.fori_loop(1, cols, share, 0)
-
-    sides_wait(kappa_ref, kb, k_send, k_recv)
-    strip = 4 * CY
-
-    def laid(ref, get, every):
-        for n, (dr, dc) in enumerate(every):
-            value = get(dr, dc)
-            for x in range(CX):
-                at_row = ((dr + 1) * CX + x) * strip + (dc + 1) * CY
-                ref[at_row : at_row + CY, :] = value[x * CY : (x + 1) * CY, :]
-
-    every = SIDES + [(0, 0)]
-
-    def valid(dr, dc):
-        return (r + dr >= 0) & (r + dr < rows) & (c + dc >= 0) & (c + dc < cols)
-
-    def stiffness(dr, dc):
-        if (dr, dc) == (0, 0):
-            return (6.0 + kappa_ref[...]) * 0.125
-        return jnp.where(valid(dr, dc), (6.0 + kb[SIDES.index((dr, dc))]) * 0.125, 0.0)
-
-    laid(coef, stiffness, every)
-    laid(
-        scale,
-        lambda dr, dc: jnp.full((cells, LANES), jnp.where(valid(dr, dc), 0.125, 0.0), F32),
-        every,
-    )
-    metas = settle(rm, devices - 1, m_sem)
-    metas.wait_recv()
-    for s in range(devices):
-        lane_hot[:, s * LANES : (s + 1) * LANES] = (rm[s, 1:2, :] == lane_rows).astype(BF16)
+    exchange(msend, rm, m_sem)
+    own_kappa.wait()
+    sides_start(kappa_ref, kb, k_send, k_recv)
 
     shares = settle(rs, cols - 1, rs_sem)
     shares.wait_recv()
@@ -283,6 +252,37 @@
     for v in range(nvec):
         vsend[:, v, :] = packed[v * devices : (v + 1) * devices]
     exchange(vsend, rv, v_sem)
+    sides_wait(kappa_ref, kb, k_send, k_recv)
+    strip = 4 * CY
+
+    def laid(ref, get, every):
+        for n, (dr, dc) in enumerate(every):
+            value = get(dr, dc)
+            for x in range(CX):
+                at_row = ((dr + 1) * CX + x) * strip + (dc + 1) * CY
+                ref[at_row : at_row + CY, :] = value[x * CY : (x + 1) * CY, :]
+
+    every = SIDES + [(0, 0)]
+
+    def valid(dr, dc):
+        return (r + dr >= 0) & (r + dr < rows) & (c + dc >= 0) & (c + dc < cols)
+
+    def stiffness(dr, dc):
+        if (dr, dc) == (0, 0):
+            return (6.0 + kappa_ref[...]) * 0.125
+        return jnp.where(valid(dr, dc), (6.0 + kb[SIDES.index((dr, dc))]) * 0.125, 0.0)
+
+    laid(coef, stiffness, every)
+    laid(
+        scale,
+        lambda dr, dc: jnp.full((cells, LANES), jnp.where(valid(dr, dc), 0.125, 0.0), F32),
+        every,
+    )
+    metas = settle(rm, devices - 1, m_sem)
+    metas.wait_recv()
+    for s in range(devices):
+        lane_hot[:, s * LANES : (s + 1) * LANES] = (rm[s, 1:2, :] == lane_rows).astype(BF16)
+
     values = settle(rv, devices - 1, v_sem)
     values.wait_recv()
 
@@ -327,8 +327,7 @@
             low = (step + 1) * strip
             span = slice(low, ext.shape[1] - low)
             cur = coef[span, :] * mid - scale[span, :] * beside
-        for x in range(CX):
-            out_ref[v, x * CY : (x + 1) * CY, :] = cur[x * strip + CY : x * strip + 2 * CY]
+        out_ref[v] = cur.reshape(CX, strip, LANES)
 
 
 def per_device(
@@ -348,10 +347,12 @@
     dma = pltpu.SemaphoreType.DMA
     out = pl.pallas_call(
         functools.partial(kernel, rows, cols, kmax, leaf),
-        out_shape=jax.ShapeDtypeStruct((nvec, cells, lanes), F32),
-        in_specs=[vmem, hbm, hbm, smem, hbm, smem, vmem, vmem],
+        out_shape=jax.ShapeDtypeStruct((nvec, CX, strip, lanes), F32),
+        in_specs=[hbm, hbm, hbm, smem, hbm, smem, hbm, hbm],
         out_specs=vmem,
         scratch_shapes=[
+            pltpu.VMEM((points // LANES, LANES), jnp.int32),
+            pltpu.VMEM((cells, lanes), F32),
             pltpu.VMEM((taps, tile), BF16),
             pltpu.VMEM((taps, tile), BF16),
             pltpu.VMEM((nleaf, leaf, leaf), BF16),
@@ -371,7 +372,7 @@
             pltpu.VMEM((nvec, deep, lanes), F32),
             pltpu.VMEM((deep, lanes), F32),
             pltpu.VMEM((deep, lanes), F32),
-            dma((3,)), dma((2,)), dma((2,)), dma((2,)), dma((2,)),
+            dma((6,)), dma((2,)), dma((2,)), dma((2,)), dma((2,)),
             dma((len(SIDES),)), dma((len(SIDES),)), dma((len(SIDES),)), dma((len(SIDES),)),
         ],
         compiler_params=pltpu.CompilerParams(collective_id=0, has_side_effects=True),
@@ -381,11 +382,11 @@
         lr_left.reshape(taps, tile),
         tile_rank.reshape(tiles),
         leaf_values.reshape(nleaf, leaf, leaf),
-        leaf_places.reshape(2 * nleaf),
+        leaf_places.reshape(nleaf, 2).T,
         cluster_perm.reshape(-1, LANES),
         kappa.reshape(cells, lanes),
     )
-    return out.reshape(nvec, CX, CY, lanes)
+    return out[:, :, CY : 2 * CY, :]
 
 
 def solution(mesh):

time: 30.7 us -> 28.3 us (0.922)
  local copies, waits for them, and re-layouts: 2.67 us -> 1.37 us
  Pallas kernels: 27.7 us -> 26.7 us
    unnamed x2 -> x0, local copies, waits for them, and re-layouts: 2.08 us -> none
    slice x0 -> x1, local copies, waits for them, and re-layouts: none -> 1.37 us  [per_device(): return out[:, :, CY:2 * CY, :]]
    pallas_call x1, Pallas kernels: 27.7 us -> 26.7 us  [per_device(): pl.pallas_call(functools.partial(kernel, rows, cols, kmax, leaf), out_sha...]
    reshape x1 -> x0, local copies, waits for them, and re-layouts: 0.59 us -> none  [per_device(): leaf_places.reshape(2 * nleaf)]
where the time goes in v2:
time: 28.3 us; the launch traced here: 28 us
  Pallas kernels  26.7 us (94%)
  local copies, waits for them, and re-layouts  1.37 us (5%)
    pallas_call x1, Pallas kernels, per_device(): pl.pallas_call(functools.partial(kernel, rows, cols, kmax, leaf), out_sha...  26.7 us
    slice x1, local copies, waits for them, and re-layouts, per_device(): return out[:, :, CY:2 * CY, :]  1.37 us

profile of v2, /device:TPU:0, one launch (start us, length us, event | category | flops | bytes accessed | tf_op | source)
XLA Modules:
  0.0 28.0 jit_solution(3325833042513919352)
XLA Ops:
  0.0 26.7 %shard_map.82 = f32[2,4,16,128]{3,2,1,0:T(8,128)} custom-call(bf16[2,2048]{1,0:T(2,128)(2,1)} %bitcast.14, bf16[256,2048]{1,0:T(8,128)(2,1)} %bitcast.11, bf16[256,2048]{1,0:T(8,128)(2,1)} %bitcast.12, s32[32]{0:T(128)} %bitcast.17, bf16[8,512,512]{2,1,0:T(8,128)(2,1)} %bitcast.10, s32[2,8]{1,0:T(2,128)} %bitcast.16, s32[64,128]{1,0:T(8,128)} %bitcast.13, ...), custom_call_target="tpu_custom_call" | custom-call | tf_op jit(solution)/shard_map/pallas_call | solution.py:348
  26.7 1.4 %slice.3 = f32[2,4,4,128]{3,2,1,0:T(4,128)} slice(f32[2,4,16,128]{3,2,1,0:T(8,128)} %shard_map.82), slice={[0:2], [0:4], [4:8], [0:128]} | slice | bytes 32768 | tf_op jit(solution)/shard_map/slice | solution.py:389

commit v3 on v2

--- a/solution.py
+++ b/solution.py
@@ -36,9 +36,9 @@
 
 def kernel(
     rows, cols, kmax, leaf,
-    x_hbm, right_hbm, left_hbm, rank_ref, leaf_hbm, places_ref, perm_hbm, kappa_hbm,
+    x_hbm, right_hbm, left_hbm, rank_hbm, leaf_hbm, places_hbm, perm_hbm, kappa_hbm,
     out_ref,
-    perm_ref, kappa_ref, right_ref, left_ref, leaf_ref, xg, x32, part, rs, slot_hot,
+    rank_ref, places_ref, near_ref, corner, hc, perm_ref, kappa_ref, right_ref, left_ref, leaf_ref, xg, x32, part, rs, slot_hot,
     msend, rm, vsend, rv, lane_hot, brick, hb, kb, ext, coef, scale,
     local_sem, ag_sem, m_sem, rs_sem, v_sem, k_send, k_recv, h_send, h_recv,
 ):
@@ -58,6 +58,10 @@
         perm_hbm.at[pl.ds(pl.multiple_of(c * blocks, 8), blocks)], perm_ref, local_sem.at[4]
     )
     own_kappa = pltpu.make_async_copy(kappa_hbm, kappa_ref, local_sem.at[5])
+    small = [
+        pltpu.make_async_copy(rank_hbm, rank_ref, local_sem.at[6]),
+        pltpu.make_async_copy(places_hbm, places_ref, local_sem.at[7]),
+    ]
     loads = [
         pltpu.make_async_copy(right_hbm, right_ref, local_sem.at[0]),
         pltpu.make_async_copy(left_hbm, left_ref, local_sem.at[1]),
@@ -77,7 +81,7 @@
         pl.semaphore_signal(
             barrier, inc=1, device_id={"row": r, "col": turned(c, k, cols)}, device_id_type=MESH
         )
-    for load in [own_x, own_perm, own_kappa] + loads:
+    for load in [own_x, own_perm] + small + [own_kappa] + loads:
         load.start()
     own_x.wait()
     pl.semaphore_wait(barrier, rows + cols - 2)
@@ -119,6 +123,27 @@
     for h in range(2):
         msend[:, h, :] = meta[h * devices : (h + 1) * devices]
 
+    for load in small:
+        load.wait()
+    wide = TILE_COLS * nvec
+    lane = iota((1, taps), 1)
+    lane_tile, lane_k = lane // kmax, lane % kmax
+    ranks = jnp.zeros((1, taps), jnp.int32)
+    for t in range(TILE_ROWS * TILE_COLS):
+        ranks = jnp.where(lane_tile == t, rank_ref[t], ranks)
+    keep = (lane_tile % TILE_COLS == iota((wide, taps), 0) // nvec) & (lane_k < ranks)
+    tall = TILE_ROWS * nvec
+    fold = (iota((tall, wide), 0) % nvec == iota((tall, wide), 1) % nvec).astype(BF16)
+    own_row = lane_tile // TILE_COLS == iota((tall, taps), 0) // nvec
+    picks = nleaf * nvec
+    row_leaves = cols * points // leaf
+    order = iota((1, 3 * picks), 1) % picks
+    row_of = jnp.zeros((1, 3 * picks), jnp.int32)
+    for l in range(nleaf):
+        row_of = jnp.where(order // nvec == l, places_ref[0, l], row_of)
+    chosen = iota((row_leaves * nvec, 3 * picks), 0)
+    selector = ((chosen // nvec == row_of) & (chosen % nvec == order % nvec)).astype(BF16)
+
     ext[...] = jnp.zeros_like(ext)
     coef[...] = jnp.zeros_like(coef)
     scale[...] = jnp.zeros_like(scale)
@@ -149,52 +174,57 @@
         ok = (rr >= 0) & (rr < rows) & (cc >= 0) & (cc < cols)
         return ok, {"row": jnp.clip(rr, 0, rows - 1), "col": jnp.clip(cc, 0, cols - 1)}
 
-    def side_copy(src, dst, send, recv, n, incoming):
+    def side_copy(pick, send, recv, n, incoming):
         slot = n if incoming else len(SIDES) - 1 - n
+        src, dst = pick(n, slot)
         return pltpu.make_async_remote_copy(
-            src_ref=src, dst_ref=dst.at[slot], send_sem=send.at[n], recv_sem=recv.at[slot],
+            src_ref=src, dst_ref=dst, send_sem=send.at[n], recv_sem=recv.at[slot],
             device_id=side(n)[1], device_id_type=MESH,
         )
 
-    def sides_start(src, dst, send, recv):
+    def sides_start(pick, send, recv):
         for n in range(len(SIDES)):
             @pl.when(side(n)[0])
             def _():
-                side_copy(src, dst, send, recv, n, False).start()
-
-    def sides_wait(src, dst, send, recv):
+                side_copy(pick, send, recv, n, False).start()
+
+    def sides_wait(pick, send, recv):
         for n in range(len(SIDES)):
             @pl.when(side(n)[0])
             def _():
-                side_copy(src, dst, send, recv, n, True).wait_recv()
-                side_copy(src, dst, send, recv, n, False).wait_send()
+                side_copy(pick, send, recv, n, True).wait_recv()
+                side_copy(pick, send, recv, n, False).wait_send()
+
+    def kappa_sides(n, slot):
+        return kappa_ref, kb.at[slot]
+
+    def field_sides(n, slot):
+        if 0 in SIDES[n]:
+            return brick, hb.at[slot]
+        return corner.at[n], hc.at[slot]
+
+    def corner_cells(dr, dc):
+        far_x = [CX - x if dr > 0 else x + 1 for x in range(CX)]
+        far_y = [CY - y if dc > 0 else y + 1 for y in range(CY)]
+        return [(x, y) for x in range(CX) for y in range(CY) if far_x[x] + far_y[y] <= 4]
 
     gathered = settle(xg, rows - 1, ag_sem)
     gathered.wait_recv()
+    own_kappa.wait()
+    sides_start(kappa_sides, k_send, k_recv)
     per = tile // points
     for s in range(rows):
         b, j = s // per, s % per
         x32[nvec * b : nvec * (b + 1), j * points : (j + 1) * points] = xg[s].astype(F32)
     loads[0].wait()
-    wide = TILE_COLS * nvec
     projected = dot_nt(x32[...].astype(BF16), right_ref[...])
-    lane = iota((1, taps), 1)
-    lane_tile, lane_k = lane // kmax, lane % kmax
-    ranks = jnp.zeros((1, taps), jnp.int32)
-    for t in range(TILE_ROWS * TILE_COLS):
-        ranks = jnp.where(lane_tile == t, rank_ref[t], ranks)
-    keep = (lane_tile % TILE_COLS == iota((wide, taps), 0) // nvec) & (lane_k < ranks)
     projected = jnp.where(keep, projected, 0.0).astype(BF16)
-    tall = TILE_ROWS * nvec
-    fold = (iota((tall, wide), 0) % nvec == iota((tall, wide), 1) % nvec).astype(BF16)
     spread_out = jnp.dot(fold, projected, preferred_element_type=F32)
-    own_row = lane_tile // TILE_COLS == iota((tall, taps), 0) // nvec
     spread_out = jnp.where(own_row, spread_out, 0.0).astype(BF16)
     loads[1].wait()
     far = jnp.dot(spread_out, left_ref[...], preferred_element_type=F32)
     loads[2].wait()
     subs = points // leaf
-    near = []
     for l in range(nleaf):
         column = places_ref[1, l]
         held = xg[column // subs].astype(F32)
@@ -202,15 +232,17 @@
         pick = jnp.zeros((nvec, leaf), F32)
         for q in range(subs):
             pick += jnp.where(sub == q, 1.0, 0.0) * held[:, q * leaf : (q + 1) * leaf]
-        near.append(dot_nt(pick.astype(BF16), leaf_ref[l]))
+        near_ref[nvec * l : nvec * (l + 1), :] = dot_nt(pick.astype(BF16), leaf_ref[l])
+    near = jnp.concatenate(pieces(near_ref[...]), axis=0).astype(BF16)
+    near = jnp.dot(selector, near, preferred_element_type=F32)
     for d in range(cols):
         a, start = d * points // tile, d * points % tile
         for q in range(subs):
-            total = far[nvec * a : nvec * (a + 1), start + q * leaf : start + (q + 1) * leaf]
-            for l in range(nleaf):
-                total += jnp.where(places_ref[0, l] == d * subs + q, 1.0, 0.0) * near[l]
-            part[d, :, q * leaf : (q + 1) * leaf] = total
-
+            at_row = nvec * (d * subs + q)
+            part[d, :, q * leaf : (q + 1) * leaf] = (
+                far[nvec * a : nvec * (a + 1), start + q * leaf : start + (q + 1) * leaf]
+                + near[at_row : at_row + nvec]
+            )
     for k in range(1, cols):
         to = turned(c, k, cols)
         pltpu.make_async_remote_copy(
@@ -218,8 +250,6 @@
             recv_sem=rs_sem.at[1], device_id={"row": r, "col": to}, device_id_type=MESH,
         ).start()
     exchange(msend, rm, m_sem)
-    own_kappa.wait()
-    sides_start(kappa_ref, kb, k_send, k_recv)
 
     shares = settle(rs, cols - 1, rs_sem)
     shares.wait_recv()
@@ -252,7 +282,7 @@
     for v in range(nvec):
         vsend[:, v, :] = packed[v * devices : (v + 1) * devices]
     exchange(vsend, rv, v_sem)
-    sides_wait(kappa_ref, kb, k_send, k_recv)
+    sides_wait(kappa_sides, k_send, k_recv)
     strip = 4 * CY
 
     def laid(ref, get, every):
@@ -302,12 +332,19 @@
     field = field[:size] + field[size : 2 * size] + field[2 * size :]
     for v in range(nvec):
         brick[v] = field[v * cells : (v + 1) * cells]
-    sides_start(brick, hb, h_send, h_recv)
+    corners = [n for n in range(len(SIDES)) if 0 not in SIDES[n]]
+    for n in corners:
+        held = corner_cells(*SIDES[n])
+        for v in range(nvec):
+            for i, (x, y) in enumerate(held):
+                j, cell = v * len(held) + i, v * cells + x * CY + y
+                corner[n, j // 4, j % 4 : j % 4 + 1, :] = field[cell : cell + 1]
+    sides_start(field_sides, h_send, h_recv)
     gathered.wait_send()
     metas.wait_send()
     shares.wait_send()
     values.wait_send()
-    sides_wait(brick, hb, h_send, h_recv)
+    sides_wait(field_sides, h_send, h_recv)
 
     def bricks(v, dr, dc):
         if (dr, dc) == (0, 0):
@@ -315,7 +352,20 @@
         return jnp.where(valid(dr, dc), hb[SIDES.index((dr, dc)), v], 0.0)
 
     for v in range(nvec):
-        laid(ext.at[v], functools.partial(bricks, v), every)
+        laid(
+            ext.at[v],
+            functools.partial(bricks, v),
+            [near_side for near_side in every if 0 in near_side],
+        )
+        for n in corners:
+            dr, dc = SIDES[n]
+            held = corner_cells(-dr, -dc)
+            for i, (x, y) in enumerate(held):
+                j = v * len(held) + i
+                at_row = ((dr + 1) * CX + x) * strip + (dc + 1) * CY + y
+                ext[v, at_row : at_row + 1, :] = jnp.where(
+                    valid(dr, dc), hc[n, j // 4, j % 4 : j % 4 + 1, :], 0.0
+                )
         cur = ext[v]
         for step in range(4):
             mid = cur[strip:-strip]
@@ -342,15 +392,19 @@
     taps = tiles * kmax
     strip, deep = 4 * CY, 3 * CX * 4 * CY
     vmem = pl.BlockSpec(memory_space=pltpu.VMEM)
-    smem = pl.BlockSpec(memory_space=pltpu.SMEM)
     hbm = pl.BlockSpec(memory_space=pl.ANY)
     dma = pltpu.SemaphoreType.DMA
     out = pl.pallas_call(
         functools.partial(kernel, rows, cols, kmax, leaf),
-        out_shape=jax.ShapeDtypeStruct((nvec, CX, strip, lanes), F32),
-        in_specs=[hbm, hbm, hbm, smem, hbm, smem, hbm, hbm],
+        out_shape=pltpu.VMEM((nvec, CX, strip, lanes), F32),
+        in_specs=[hbm] * 8,
         out_specs=vmem,
         scratch_shapes=[
+            pltpu.SMEM((tiles,), jnp.int32),
+            pltpu.SMEM((2, nleaf), jnp.int32),
+            pltpu.VMEM((nleaf * nvec, leaf), F32),
+            pltpu.VMEM((len(SIDES), 3 * nvec // 2, 4, lanes), F32),
+            pltpu.VMEM((len(SIDES), 3 * nvec // 2, 4, lanes), F32),
             pltpu.VMEM((points // LANES, LANES), jnp.int32),
             pltpu.VMEM((cells, lanes), F32),
             pltpu.VMEM((taps, tile), BF16),
@@ -372,7 +426,7 @@
             pltpu.VMEM((nvec, deep, lanes), F32),
             pltpu.VMEM((deep, lanes), F32),
             pltpu.VMEM((deep, lanes), F32),
-            dma((6,)), dma((2,)), dma((2,)), dma((2,)), dma((2,)),
+            dma((8,)), dma((2,)), dma((2,)), dma((2,)), dma((2,)),
             dma((len(SIDES),)), dma((len(SIDES),)), dma((len(SIDES),)), dma((len(SIDES),)),
         ],
         compiler_params=pltpu.CompilerParams(collective_id=0, has_side_effects=True),

time: 28.3 us -> 25.6 us (0.905)
  Pallas kernels: 26.7 us -> 24.8 us
  local copies, waits for them, and re-layouts: 1.37 us -> 0.61 us
    pallas_call x1, Pallas kernels: 26.7 us -> 24.8 us  [per_device(): pl.pallas_call(functools.partial(kernel, rows, cols, kmax, leaf), out_sha...]
    slice x1, local copies, waits for them, and re-layouts: 1.37 us -> 0.61 us  [per_device(): return out[:, :, CY:2 * CY, :]]
where the time goes in v3:
time: 25.6 us; the launch traced here: 25.4 us
  Pallas kernels  24.8 us (97%)
  local copies, waits for them, and re-layouts  0.61 us (2%)
    pallas_call x1, Pallas kernels, per_device(): pl.pallas_call(functools.partial(kernel, rows, cols, kmax, leaf), out_sha...  24.8 us
    slice x1, local copies, waits for them, and re-layouts, per_device(): return out[:, :, CY:2 * CY, :]  0.61 us

profile of v3, /device:TPU:0, one launch (start us, length us, event | category | flops | bytes accessed | tf_op | source)
XLA Modules:
  0.0 25.4 jit_solution(2068833002073350495)
XLA Ops:
  0.0 24.8 %shard_map.82 = f32[2,4,16,128]{3,2,1,0:T(8,128)S(1)} custom-call(bf16[2,2048]{1,0:T(2,128)(2,1)} %bitcast.14, bf16[256,2048]{1,0:T(8,128)(2,1)} %bitcast.11, bf16[256,2048]{1,0:T(8,128)(2,1)} %bitcast.12, s32[32]{0:T(128)} %bitcast.17, bf16[8,512,512]{2,1,0:T(8,128)(2,1)} %bitcast.10, s32[2,8]{1,0:T(2,128)} %bitcast.16, s32[64,128]{1,0:T(8,128)} %bitcast.13, ...), custom_call_target="tpu_custom_call" | custom-call | tf_op jit(solution)/shard_map/pallas_call | solution.py:397
  24.8 0.6 %slice.3 = f32[2,4,4,128]{3,2,1,0:T(4,128)} slice(f32[2,4,16,128]{3,2,1,0:T(8,128)S(1)} %shard_map.82), slice={[0:2], [0:4], [4:8], [0:128]} | slice | bytes 32768 | tf_op jit(solution)/shard_map/slice | solution.py:443
